TPU v7x, 32 devices: a whole 2x2x4 slice. The times are simulated.
32 devices in a mesh: row: 4 (over y, core), col: 8 (over z, x).
Axes of the slice: x: 2, y: 2, z: 4, core: 2. Of those that a mesh axis runs over, the one named last changes fastest.
Arguments:
- demand: bfloat16 [12288, 128], P(('row', 'col')), may hold values from -6 to 6
- tile_data: bfloat16 [4, 8, 128, 128, 128], P('row', 'col'), may hold values from -0.078125 to 0.078125
- tile_row: int32 [4, 8, 128], P('row', 'col'), may hold values from 0 to 12, as said below
- tile_col: int32 [4, 8, 128], P('row', 'col'), may hold values from 0 to 23, as said below
Outputs:
- leontief: bfloat16 [12288, 128], P(('row', 'col'))
Inputs may be any that keep to these rules, and one draw needn't show every extreme that they name: `tile_row`: the value 4 * 3 marks an empty slot. In every index pair the live slots come first and number at least 42; in every draw some index pair has all 128 slots live. Two slots may name the same tile position; their tiles then add. `tile_col`: empty slots carry a column too, which is ignored.
All inputs are finite; a program needn't handle non-finite values.
Results may differ from a plain program's by a relative error of at most 0.018.
Values may be sent and summed in bfloat16 or wider, within the bound.
A program may use at most 64 MiB of HBM per device.

v0:
```python
import jax
import jax.numpy as jnp
from jax import lax
from jax.sharding import PartitionSpec as P


def multiply(panel_piece, tile_block, slot_rows, slot_cols):
    edge = tile_block.shape[-1]
    columns = panel_piece.shape[1]
    slot_count = tile_block.shape[0]
    local_rows = lax.axis_size("row") * (panel_piece.shape[0] // edge)
    gathered = lax.all_gather(panel_piece, "col", axis=0, tiled=True)
    blocks = gathered.reshape(-1, edge, columns)
    picked = jnp.take(blocks, slot_cols, axis=0)
    products = jnp.einsum("stk,skc->stc", tile_block, picked, preferred_element_type=jnp.float32)
    products = products.reshape(slot_count, -1)
    upper = products.astype(jnp.bfloat16)
    lower = (products - upper.astype(jnp.float32)).astype(jnp.bfloat16)
    targets = jnp.arange(local_rows, dtype=jnp.int32)
    onehot = (slot_rows[None, :] == targets[:, None]).astype(jnp.bfloat16)
    partial_value = jnp.dot(onehot, upper, preferred_element_type=jnp.float32)
    partial_value = partial_value + jnp.dot(onehot, lower, preferred_element_type=jnp.float32)
    partial_value = lax.optimization_barrier(partial_value.astype(jnp.bfloat16)).astype(jnp.float32)
    partial_value = partial_value.reshape(local_rows * edge, columns)
    summed = lax.psum_scatter(
        partial_value.astype(jnp.bfloat16), "row", scatter_dimension=0, tiled=True
    )
    return summed


def body(demand, tile_data, tile_row, tile_col):
    tile_block = tile_data[0, 0]
    slot_rows = tile_row[0, 0]
    slot_cols = tile_col[0, 0]
    first_term = multiply(demand, tile_block, slot_rows, slot_cols)
    second_term = multiply(first_term, tile_block, slot_rows, slot_cols)
    summed = (
        demand.astype(jnp.float32)
        + first_term.astype(jnp.float32)
        + second_term.astype(jnp.float32)
    )
    return summed.astype(jnp.bfloat16)


def solution(mesh):
    placed = (
        P(("row", "col"), None),
        P("row", "col", None, None, None),
        P("row", "col", None),
        P("row", "col", None),
    )
    return jax.shard_map(
        body, mesh=mesh, in_specs=placed, out_specs=P(("row", "col"), None), check_vma=False
    )
```

profile of v0, /device:TPU:0, one launch (start us, length us, event | category | flops | bytes accessed | tf_op | source)
XLA Modules:
  0.0 185.6 jit_solution(8548706937118380226)
XLA Ops:
  6.5 0.0 reduce-scatter.3.cloned.1.call-start
  6.5 0.7 compare_and_fusion
  7.2 0.7 compare_select_fusion
  7.9 34.1 %all_gather.6 = bf16[3072,128]{1,0:T(8,128)(2,1)S(1)} all-gather(bf16[384,128]{1,0:T(8,128)(2,1)} %param.6), channel_id=1, replica_groups=mesh['row'=4,'col'=8] {'col'}, dimensions={0}, use_global_device_ids=true | all-gather | bytes 884736 | tf_op jit(solution)/shard_map/all_gather | solution.py:12
  41.9 3.0 %gather_fusion = bf16[128,128,128]{2,1,0:T(8,128)(2,1)} fusion(bf16[24,128,128]{2,1,0:T(8,128)(2,1)S(1)} %bitcast.37, s32[1024]{0:T(1024)S(1)} %pad_clamp_fusion), kind=kCustom, calls=%fused_computation.clone | custom fusion | bytes 8389120 | tf_op jit(solution)/shard_map/jit(_take)/gather | solution.py:14
  45.0 9.9 %fusion.12 = f32[128,128,128]{1,2,0:T(8,128)} fusion(bf16[1,1,128,128,128]{4,3,2,1,0:T(8,128)(2,1)} %param.7, bf16[128,128,128]{2,1,0:T(8,128)(2,1)} %gather_fusion, pred[128]{0:T(512)(128)(4,1)S(1)} %compare_and_fusion), kind=kOutput, calls=%fused_computation.20 | convolution fusion | flops 538968064 | bytes 16777344 | tf_op jit(solution)/shard_map/stk,skc->stc/dot_general | solution.py:15
  54.9 9.4 %copy.6 = f32[128,128,128]{0,2,1:T(8,128)} copy(f32[128,128,128]{1,2,0:T(8,128)} %fusion.12) | data formatting | bytes 16777216 | tf_op jit(solution)/shard_map/stk,skc->stc/dot_general | solution.py:15
  64.3 0.0 copy-start.2
  64.3 4.0 %fusion.3 = (bf16[128,16384]{0,1:T(8,128)(2,1)S(1)}, bf16[128,16384]{0,1:T(8,128)(2,1)S(1)}) fusion(f32[128,128,128]{0,2,1:T(8,128)} %copy.6), kind=kLoop, calls=%fused_computation.11 | loop fusion | flops 8388608 | bytes 16777216 | tf_op jit(solution)/shard_map/convert_element_type | solution.py:18
  68.4 0.0 copy-done.2
  68.4 1.2 fusion.25
  69.6 1.2 fusion
  70.8 1.1 convert_element_type.53
  71.9 0.0 reduce-scatter.3.cloned.1.call-update
  71.9 0.0 reduce-scatter.5.cloned.1.call-start
  71.9 21.8 %reduce-scatter.3.cloned.1.call-done = bf16[384,128]{1,0:T(8,128)(2,1)} async-done(((bf16[1536,128]{1,0:T(8,128)(2,1)}), bf16[384,128]{1,0:T(8,128)(2,1)}) %reduce-scatter.3.cloned.1.call-update) | async-done | bytes 98320 | tf_op jit(solution)/shard_map/reduce_scatter | solution.py:25
  93.8 32.4 %all_gather.7 = bf16[3072,128]{1,0:T(8,128)(2,1)S(1)} all-gather(bf16[384,128]{1,0:T(8,128)(2,1)} %reduce-scatter.3.cloned.1.call-done), channel_id=1, replica_groups=mesh['row'=4,'col'=8] {'col'}, dimensions={0}, use_global_device_ids=true | all-gather | bytes 884736 | tf_op jit(solution)/shard_map/all_gather | solution.py:12
  126.2 3.0 %gather_fusion.1 = bf16[128,128,128]{2,1,0:T(8,128)(2,1)} fusion(bf16[24,128,128]{2,1,0:T(8,128)(2,1)S(1)} %bitcast.36, s32[1024]{0:T(1024)S(1)} %pad_clamp_fusion), kind=kCustom, calls=%fused_computation.1.clone | custom fusion | bytes 8389120 | tf_op jit(solution)/shard_map/jit(_take)/gather | solution.py:14
  129.3 9.9 %fusion.17 = f32[128,128,128]{1,2,0:T(8,128)} fusion(bf16[1,1,128,128,128]{4,3,2,1,0:T(8,128)(2,1)} %param.7, bf16[128,128,128]{2,1,0:T(8,128)(2,1)} %gather_fusion.1, pred[128]{0:T(512)(128)(4,1)S(1)} %compare_and_fusion), kind=kOutput, calls=%fused_computation.21 | convolution fusion | flops 538968064 | bytes 16777344 | tf_op jit(solution)/shard_map/stk,skc->stc/dot_general | solution.py:15
  139.2 9.4 %copy.8 = f32[128,128,128]{0,2,1:T(8,128)} copy(f32[128,128,128]{1,2,0:T(8,128)} %fusion.17) | data formatting | bytes 16777216 | tf_op jit(solution)/shard_map/stk,skc->stc/dot_general | solution.py:15
  148.6 4.0 %fusion.2 = (bf16[128,16384]{0,1:T(8,128)(2,1)S(1)}, bf16[128,16384]{0,1:T(8,128)(2,1)S(1)}) fusion(f32[128,128,128]{0,2,1:T(8,128)} %copy.8), kind=kLoop, calls=%fused_computation.8 | loop fusion | flops 8388608 | bytes 16777216 | tf_op jit(solution)/shard_map/convert_element_type | solution.py:18
  152.6 1.2 fusion.24
  153.8 0.0 copy-start
  153.8 0.0 copy-start.1
  153.8 1.2 fusion.1
  155.0 1.1 convert_element_type.59
  156.1 0.0 reduce-scatter.5.cloned.1.call-update
  156.1 21.1 %reduce-scatter.5.cloned.1.call-done = bf16[384,128]{1,0:T(8,128)(2,1)} async-done(((bf16[1536,128]{1,0:T(8,128)(2,1)}), bf16[384,128]{1,0:T(8,128)(2,1)}) %reduce-scatter.5.cloned.1.call-update) | async-done | bytes 98320 | tf_op jit(solution)/shard_map/reduce_scatter | solution.py:25
  177.2 0.0 copy-done
  177.2 0.0 copy-done.1
  177.2 1.6 add_convert_fusion
  (1 shorter events, 0.0 us)
Async XLA Ops:
  6.5 87.2 %reduce-scatter.3.cloned.1.call-start = ((), (), s32[]{:S(2)}) async-start(), calls=%async_computation.2 | async-start | bytes 491520 | tf_op jit(solution)/shard_map/reduce_scatter | solution.py:25
  64.3 4.0 %copy-start.2 = (s32[1,1,128]{2,1,0:T(1,128)S(1)}, s32[1,1,128]{2,1,0:T(1,128)}, u32[]{:S(2)}) copy-start(s32[1,1,128]{2,1,0:T(1,128)} %param.8) | copy-start | bytes 1540
  71.9 105.3 %reduce-scatter.5.cloned.1.call-start = ((), (), s32[]{:S(2)}) async-start(), calls=%async_computation.3 | async-start | bytes 491520 | tf_op jit(solution)/shard_map/reduce_scatter | solution.py:25
  153.8 23.4 %copy-start = (bf16[384,128]{1,0:T(8,128)(2,1)S(1)}, bf16[384,128]{1,0:T(8,128)(2,1)}, u32[]{:S(2)}) copy-start(bf16[384,128]{1,0:T(8,128)(2,1)} %param.6) | copy-start | bytes 294916
  153.8 23.4 %copy-start.1 = (bf16[384,128]{1,0:T(8,128)(2,1)S(1)}, bf16[384,128]{1,0:T(8,128)(2,1)}, u32[]{:S(2)}) copy-start(bf16[384,128]{1,0:T(8,128)(2,1)} %reduce-scatter.3.cloned.1.call-done) | copy-start | bytes 294916
Sparse Core Ops, SparseCore 0:
  72.0 21.7 reduce-scatter.2
  156.3 20.8 reduce-scatter.4
where the time goes:
time: 186 us
  blocking collectives  66.5 us (36%)
  waiting for transfers between devices  42.9 us (23%)
  local copies, waits for them, and re-layouts  27.1 us (15%)
  matrix products  24.6 us (13%)
  between operations  13.4 us (7%)
  other arithmetic  11 us (6%)
    all_gather x2, blocking collectives, multiply(): gathered = lax.all_gather(panel_piece, 'col', axis=0, tiled=True)  66.5 us
    reduce_scatter x2, waiting for transfers between devices, multiply(): lax.psum_scatter(partial_value.astype(jnp.bfloat16), 'row', scatter_dimen...  42.9 us
    dot_general x2, matrix products, multiply(): jnp.einsum('stk,skc->stc', tile_block, picked, preferred_element_type=jnp...  19.8 us
    dot_general x2, local copies, waits for them, and re-layouts, multiply(): jnp.einsum('stk,skc->stc', tile_block, picked, preferred_element_type=jnp...  18.8 us
    convert_element_type x2, other arithmetic, multiply(): lower = (products - upper.astype(jnp.float32)).astype(jnp.bfloat16)  8.06 us
    gather x2, local copies, waits for them, and re-layouts, multiply(): picked = jnp.take(blocks, slot_cols, axis=0)  6.08 us
  transfers between devices with their start and end apart: 2, of which 2 were waited for; matrix products, arithmetic and copies ran while one was open for 0% of the time, Pallas kernels for 0%

commit v1 on v0

v1 whole, which is shorter than its diff:
```python
import functools

import jax
import jax.numpy as jnp
from jax import lax
from jax.experimental import pallas as pl
from jax.experimental.pallas import tpu as pltpu
from jax.sharding import PartitionSpec as P

GROUP = 2
UNROLL = 10
MESH = pl.DeviceIdType.MESH


def schedule(slot_rows, slot_cols, local_rows, zero_block, units):
    slots = slot_rows.shape[0]
    index = jnp.arange(slots, dtype=jnp.int32)
    same = slot_rows[:, None] == slot_rows[None, :]
    earlier = index[None, :] < index[:, None]
    live = slot_rows < local_rows
    prior = jnp.sum((same & earlier).astype(jnp.int32), axis=1)
    opens = live & (prior % GROUP == 0)
    below = slot_rows[None, :] < slot_rows[:, None]
    base = jnp.sum((below & opens[None, :]).astype(jnp.int32), axis=1)
    place = jnp.where(live, base * GROUP + prior, -1)
    spots = jnp.arange(units * GROUP, dtype=jnp.int32)
    hit = place[None, :] == spots[:, None]
    source = jnp.sum(jnp.where(hit, index[None, :], 0), axis=1)
    column = zero_block + jnp.sum(jnp.where(hit, slot_cols[None, :] - zero_block, 0), axis=1)
    heads = place[None, :] == jnp.arange(units, dtype=jnp.int32)[:, None] * GROUP
    keep = 1 - jnp.sum((heads & (prior == 0)[None, :]).astype(jnp.int32), axis=1)
    targets = jnp.arange(local_rows, dtype=jnp.int32)
    mine = slot_rows[None, :] == targets[:, None]
    last = jnp.max(jnp.where(mine, place[None, :] // GROUP, -1), axis=1)
    last = jnp.where(last < 0, units, last)
    return jnp.concatenate([source, column, keep, last])


def kernel(n_row, n_col, n_x, units, plan, demand, tile_hbm, out, tiles, panel_a, panel_b, products,
           packed, landed, first, tile_sem, sx, rx, su, ru, sd, rd, sh, rh, sr, rr):
    n_z = n_col // n_x
    span, edge, columns = demand.shape
    zero_block = n_col * span
    spots = units * GROUP
    half = span // 2 if n_x > 1 else 0
    row = lax.axis_index("row")
    col = lax.axis_index("col")
    z = col // n_x
    x = col % n_x
    peer = z * n_x + (n_x - 1 - x)
    up_ok = z < n_z - 1
    down_ok = z > 0

    tile_copy = pltpu.make_async_copy(tile_hbm.at[0, 0], tiles, tile_sem)
    tile_copy.start()

    barrier = pltpu.get_barrier_semaphore()

    def greet(r, c):
        pl.semaphore_signal(barrier, inc=1, device_id=(r, c), device_id_type=MESH)

    for step in range(1, n_row):
        greet((row + step) % n_row, col)
    if n_x > 1:
        greet(row, peer)
    pl.when(up_ok)(lambda: greet(row, col + n_x))
    pl.when(down_ok)(lambda: greet(row, col - n_x))

    for panel in (panel_a, panel_b):
        panel[zero_block] = jnp.zeros((edge, columns), panel.dtype)
    products[units] = jnp.zeros((edge, columns), jnp.float32)
    panel_a[pl.ds(col * span, span)] = demand[...]
    greeted = n_row - 1 + (1 if n_x > 1 else 0) + up_ok.astype(jnp.int32) + down_ok.astype(jnp.int32)
    pl.semaphore_wait(barrier, greeted)

    def remote(src, dst, send, recv, target):
        return pltpu.make_async_remote_copy(
            src_ref=src, dst_ref=dst, send_sem=send, recv_sem=recv, device_id=(row, target), device_id_type=MESH
        )

    def gather(turn, own, panel):
        def block(c, start=0, stop=span):
            return panel.at[pl.ds(c * span + start, stop - start)]

        def cross(c, offset, src=None, start=0):
            at = (turn, offset + n_z - 1)
            return remote(block(c, start) if src is None else src, block(c, start), sx.at[at], rx.at[at], peer)

        def upward(c, away, src=None):
            return remote(block(c) if src is None else src, block(c), su.at[turn, away], ru.at[turn, away + 1], col + n_x)

        def downward(c, away, src=None):
            return remote(block(c) if src is None else src, block(c), sd.at[turn, away], rd.at[turn, away + 1], col - n_x)

        def side(c, way, target):
            return remote(block(c, 0, half), block(c, 0, half), sh.at[turn, way], rh.at[turn, way], target)

        pl.when(up_ok)(lambda: upward(col, 0, own).start())
        pl.when(down_ok)(lambda: downward(col, 0, own).start())
        if n_x > 1:
            cross(col, 0, own).start()
        if half:
            cross(peer, 0).wait_recv()
            pl.when(up_ok)(lambda: side(peer, 0, col + n_x).start())
            pl.when(down_ok)(lambda: side(peer, 1, col - n_x).start())
        for away in range(1, n_z):
            skip = half if away == 1 else 0

            @pl.when(z >= away)
            def _():
                c = col - away * n_x
                remote(block(c), block(c), su.at[turn, away - 1], ru.at[turn, away], col).wait_recv()
                if n_x > 1:
                    cross(c, -away, start=skip).start()
                if away + 1 < n_z:
                    pl.when(up_ok)(lambda: upward(c, away).start())

            @pl.when(z + away < n_z)
            def _():
                c = col + away * n_x
                remote(block(c), block(c), sd.at[turn, away - 1], rd.at[turn, away], col).wait_recv()
                if n_x > 1:
                    cross(c, away, start=skip).start()
                if away + 1 < n_z:
                    pl.when(down_ok)(lambda: downward(c, away).start())

        if n_x > 1:
            if half:
                pl.when(down_ok)(lambda: side(peer - n_x, 0, col).wait_recv())
                pl.when(up_ok)(lambda: side(peer + n_x, 1, col).wait_recv())
            else:
                cross(peer, 0).wait_recv()
            for away in range(1, n_z):
                skip = half if away == 1 else 0
                pl.when(z >= away)(lambda: cross(peer - away * n_x, -away, start=skip).wait_recv())
                pl.when(z + away < n_z)(lambda: cross(peer + away * n_x, away, start=skip).wait_recv())

        def drain():
            pl.when(up_ok)(lambda: upward(col, 0, own).wait_send())
            pl.when(down_ok)(lambda: downward(col, 0, own).wait_send())
            if n_x > 1:
                cross(col, 0, own).wait_send()
            if half:
                pl.when(up_ok)(lambda: side(peer, 0, col + n_x).wait_send())
                pl.when(down_ok)(lambda: side(peer, 1, col - n_x).wait_send())
            for away in range(1, n_z):
                skip = half if away == 1 else 0

                @pl.when(z >= away)
                def _():
                    c = col - away * n_x
                    if n_x > 1:
                        cross(c, -away, start=skip).wait_send()
                    if away + 1 < n_z:
                        pl.when(up_ok)(lambda: upward(c, away).wait_send())

                @pl.when(z + away < n_z)
                def _():
                    c = col + away * n_x
                    if n_x > 1:
                        cross(c, away, start=skip).wait_send()
                    if away + 1 < n_z:
                        pl.when(down_ok)(lambda: downward(c, away).wait_send())

        return drain

    def compute(panel):
        def body(step, total):
            for part in range(UNROLL):
                unit = step * UNROLL + part
                left = [tiles[plan[unit * GROUP + k]] for k in range(GROUP)]
                right = [panel[plan[spots + unit * GROUP + k]] for k in range(GROUP)]
                keep = plan[2 * spots + unit].astype(jnp.float32)
                total = total * keep + jnp.dot(
                    jnp.concatenate(left, axis=1), jnp.concatenate(right, axis=0), preferred_element_type=jnp.float32
                )
                products[unit] = total
            return total

        lax.fori_loop(0, units // UNROLL, body, jnp.zeros((edge, columns), jnp.float32))

    def scatter(turn):
        def pack(r):
            for k in range(span):
                packed[turn, r * span + k] = products[plan[2 * spots + units + r * span + k]].astype(packed.dtype)

        def send(step):
            r = (row + step) % n_row
            return pltpu.make_async_remote_copy(
                src_ref=packed.at[turn, pl.ds(r * span, span)],
                dst_ref=landed.at[turn, step - 1],
                send_sem=sr.at[turn, step - 1],
                recv_sem=rr.at[turn, step - 1],
                device_id=(r, col),
                device_id_type=MESH,
            )

        steps = sorted(range(1, n_row), key=lambda step: abs(step - n_row // 2))
        for step in steps:
            pack((row + step) % n_row)
            send(step).start()
        pack(row)
        value = packed[turn, pl.ds(row * span, span)].astype(jnp.float32)
        for step in range(1, n_row):
            send(step).wait_recv()
            value = value + landed[turn, step - 1].astype(jnp.float32)

        def drain():
            for step in range(1, n_row):
                send(step).wait_send()

        return value.astype(first.dtype), drain

    drains = [gather(0, demand, panel_a)]
    tile_copy.wait()
    compute(panel_a)
    value, drain = scatter(0)
    drains.append(drain)
    first[...] = value
    panel_b[pl.ds(col * span, span)] = value
    drains.append(gather(1, first, panel_b))
    compute(panel_b)
    value, drain = scatter(1)
    drains.append(drain)
    out[...] = (
        demand[...].astype(jnp.float32) + first[...].astype(jnp.float32) + value.astype(jnp.float32)
    ).astype(out.dtype)
    for drain in drains:
        drain()


def body(n_row, n_col, demand, tile_data, tile_row, tile_col):
    slots, edge = tile_data.shape[2], tile_data.shape[-1]
    columns = demand.shape[1]
    span = demand.shape[0] // edge
    local_rows = n_row * span
    n_x = 2 if n_col % 2 == 0 else 1
    n_z = n_col // n_x
    units = (slots + local_rows * (GROUP - 1)) // GROUP
    units = -(-units // UNROLL) * UNROLL
    plan = schedule(tile_row[0, 0], tile_col[0, 0], local_rows, n_col * span, units)
    dma = pltpu.SemaphoreType.DMA
    vmem = pl.BlockSpec(memory_space=pltpu.VMEM)
    result = pl.pallas_call(
        functools.partial(kernel, n_row, n_col, n_x, units),
        out_shape=jax.ShapeDtypeStruct((span, edge, columns), demand.dtype),
        in_specs=[pl.BlockSpec(memory_space=pltpu.SMEM), vmem, pl.BlockSpec(memory_space=pl.ANY)],
        out_specs=vmem,
        scratch_shapes=[
            pltpu.VMEM((slots, edge, edge), tile_data.dtype),
            pltpu.VMEM((n_col * span + 1, edge, columns), demand.dtype),
            pltpu.VMEM((n_col * span + 1, edge, columns), demand.dtype),
            pltpu.VMEM((units + 1, edge, columns), jnp.float32),
            pltpu.VMEM((2, local_rows, edge, columns), demand.dtype),
            pltpu.VMEM((2, n_row - 1, span, edge, columns), demand.dtype),
            pltpu.VMEM((span, edge, columns), demand.dtype),
            dma,
            dma((2, 2 * n_z - 1)),
            dma((2, 2 * n_z - 1)),
            dma((2, n_z + 1)),
            dma((2, n_z + 1)),
            dma((2, n_z + 1)),
            dma((2, n_z + 1)),
            dma((2, 2)),
            dma((2, 2)),
            dma((2, n_row - 1)),
            dma((2, n_row - 1)),
        ],
        compiler_params=pltpu.CompilerParams(
            collective_id=0, has_side_effects=True, vmem_limit_bytes=56 * 1024 * 1024
        ),
    )(plan, demand.reshape(span, edge, columns), tile_data)
    return result.reshape(demand.shape)


def solution(mesh):
    placed = (
        P(("row", "col"), None),
        P("row", "col", None, None, None),
        P("row", "col", None),
        P("row", "col", None),
    )
    return jax.shard_map(
        functools.partial(body, mesh.shape["row"], mesh.shape["col"]),
        mesh=mesh, in_specs=placed, out_specs=P(("row", "col"), None), check_vma=False,
    )
```

time: 186 us -> 57.7 us (0.31)
  blocking collectives: 66.5 us -> 0 us
  Pallas kernels: 0 us -> 49.9 us
  waiting for transfers between devices: 42.9 us -> 0 us
  local copies, waits for them, and re-layouts: 27.1 us -> 1.54 us
  matrix products: 24.6 us -> 0 us
  between operations: 13.4 us -> 0.04 us
  other arithmetic: 11 us -> 5.58 us
    all_gather x2 -> x0, blocking collectives: 66.5 us -> none  [multiply(): gathered = lax.all_gather(panel_piece, 'col', axis=0, tiled=True)]
    pallas_call x0 -> x1, Pallas kernels: none -> 49.9 us  [body(): pl.pallas_call(functools.partial(kernel, n_row, n_col, n_x, units), out_s...]
    reduce_scatter x2 -> x0, waiting for transfers between devices: 42.9 us -> none  [multiply(): lax.psum_scatter(partial_value.astype(jnp.bfloat16), 'row', scatter_dimen...]
    dot_general x6 -> x0, matrix products: 24.6 us -> none  [the longest x2 19.8 us: multiply(): jnp.einsum('stk,skc->stc', tile_block, picked, preferred_element_type=jnp...]
    dot_general x2 -> x0, local copies, waits for them, and re-layouts: 18.8 us -> none  [multiply(): jnp.einsum('stk,skc->stc', tile_block, picked, preferred_element_type=jnp...]
    convert_element_type x3 -> x0, other arithmetic: 9.63 us -> none  [the longest x2 8.06 us: multiply(): lower = (products - upper.astype(jnp.float32)).astype(jnp.bfloat16)]
    gather x2 -> x0, local copies, waits for them, and re-layouts: 6.08 us -> none  [multiply(): picked = jnp.take(blocks, slot_cols, axis=0)]
    convert_element_type x2 -> x0, local copies, waits for them, and re-layouts: 2.16 us -> none  [multiply(): partial_value.astype(jnp.bfloat16)]
  transfers between devices with their start and end apart: 2 -> 0, of which waited for: 2 -> 0; matrix products, arithmetic and copies ran while one was open for 0% -> 0% of each run, Pallas kernels for 0% -> 0%
where the time goes in v1:
time: 57.7 us; the launch traced here: 57.1 us
  Pallas kernels  49.9 us (86%)
  other arithmetic  5.58 us (10%)
  local copies, waits for them, and re-layouts  1.54 us (3%)
    pallas_call x1, Pallas kernels, body(): pl.pallas_call(functools.partial(kernel, n_row, n_col, n_x, units), out_s...  49.9 us
    unnamed x1, local copies, waits for them, and re-layouts  1.54 us

profile of v1, /device:TPU:0, one launch (start us, length us, event | category | flops | bytes accessed | tf_op | source)
XLA Modules:
  0.0 57.1 jit_solution(10154394106049708723)
XLA Ops:
  0.0 0.9 %convert_reduce_fusion.1 = s32[128]{0:T(128)S(1)} fusion(s32[128]{0:T(128)} %bitcast.10), kind=kLoop, calls=%fused_computation.4 | loop fusion | flops 81792 | bytes 1024 | tf_op jit(solution)/shard_map/reduce_sum | solution.py:21
  0.9 0.7 %add_bitcast_fusion = s32[128]{0:T(128)S(1)} fusion(s32[1,1,128]{2,1,0:T(1,128)} %param.7), kind=kLoop, calls=%fused_computation.24 | loop fusion | flops 128 | bytes 1024 | tf_op jit(solution)/shard_map/sub | solution.py:29
  1.6 0.7 %broadcast_compare_fusion = (pred[128]{0:T(512)(128)(4,1)S(1)}, pred[128]{0:T(512)(128)(4,1)S(1)}) fusion(s32[128]{0:T(128)S(1)} %convert_reduce_fusion.1, s32[1,1,128]{2,1,0:T(1,128)} %param.6), kind=kLoop, calls=%fused_computation.26 | loop fusion | flops 1920 | bytes 1280 | tf_op jit(solution)/shard_map/eq | solution.py:31
  2.2 0.9 %convert_reduce_fusion = s32[128]{0:T(128)S(1)} fusion(s32[128]{0:T(128)} %bitcast.11, pred[128]{0:T(512)(128)(4,1)S(1)} %get-tuple-element.10), kind=kLoop, calls=%fused_computation.3 | loop fusion | flops 65408 | bytes 1152 | tf_op jit(solution)/shard_map/reduce_sum | solution.py:24
  3.1 0.7 %and_select_fusion = (s32[128]{0:T(128)S(1)}, s32[128]{0:T(128)S(1)}) fusion(s32[128]{0:T(128)S(1)} %convert_reduce_fusion.1, s32[128]{0:T(128)S(1)} %convert_reduce_fusion, s32[1,1,128]{2,1,0:T(1,128)} %param.6), kind=kLoop, calls=%fused_computation.14 | loop fusion | flops 2432 | bytes 2560 | tf_op jit(solution)/shard_map/jit(floor_divide)/jit(_where)/select_n | solution.py:34
  3.8 0.2 convert_reduce_fusion.2
  4.0 0.8 %select_reduce_fusion.2 = s32[12]{0:T(128)S(1)} fusion(s32[128]{0:T(128)S(1)} %get-tuple-element.7, s32[128]{0:T(128)} %bitcast.12), kind=kLoop, calls=%fused_computation.8 | loop fusion | flops 4596 | bytes 1072 | tf_op jit(solution)/shard_map/reduce_max | solution.py:34
  4.8 0.2 select_reduce_fusion.1
  5.0 0.7 %pad_add_fusion.plan = s32[362]{0:T(512)} fusion(s32[12]{0:T(128)S(1)} %compare_select_fusion, s32[70]{0:T(128)S(1)} %broadcast_subtract_fusion, s32[140]{0:T(256)S(1)} %broadcast_add_fusion, s32[140]{0:T(256)S(1)} %get-tuple-element.5), kind=kLoop, calls=%fused_computation.13 | loop fusion | flops 1086 | bytes 2896 | tf_op jit(solution)/shard_map/concatenate | solution.py:36
  5.6 49.9 %shard_map.46 = bf16[3,128,128]{2,1,0:T(8,128)(2,1)} custom-call(s32[362]{0:T(512)} %pad_add_fusion.plan, bf16[3,128,128]{2,1,0:T(8,128)(2,1)} %bitcast.9, bf16[1,1,128,128,128]{4,3,2,1,0:T(8,128)(2,1)} %tile_hbm.1), custom_call_target="tpu_custom_call" | custom-call | tf_op jit(solution)/shard_map/pallas_call | solution.py:244
  55.5 1.5 %copy.6 = bf16[384,128]{1,0:T(8,128)(2,1)} copy(bf16[384,128]{1,0:T(8,128)(2,1)} %bitcast.8) | data formatting | bytes 196608
  (4 shorter events, 0.0 us)

commit v2 on v0

v2 whole, which is shorter than its diff:
```python
import functools

import jax
import jax.numpy as jnp
from jax import lax
from jax.experimental import pallas as pl
from jax.experimental.pallas import tpu as pltpu
from jax.sharding import PartitionSpec as P

GROUP = 2
UNROLL = 10
CUTS = 1
MESH = pl.DeviceIdType.MESH


def schedule(rows_ref, cols_ref, plan_vector, local_rows, zero_block, units):
    slots = rows_ref.shape[1]
    width = plan_vector.shape[1]
    square = (slots, slots)
    row_lane = jnp.broadcast_to(rows_ref[...], square)
    row_sub = jnp.transpose(row_lane)
    col_sub = jnp.transpose(jnp.broadcast_to(cols_ref[...], square))[:, 0:1]
    lane = lax.broadcasted_iota(jnp.int32, square, 1)
    sub = lax.broadcasted_iota(jnp.int32, square, 0)
    same = row_lane == row_sub
    prior_sub = jnp.sum(jnp.where(same & (lane < sub), 1, 0), axis=1, keepdims=True)
    prior_lane = jnp.sum(jnp.where(same & (sub < lane), 1, 0), axis=0, keepdims=True)
    opens = jnp.where((prior_lane & (GROUP - 1)) == 0, 1, 0)
    base = jnp.sum(jnp.where(row_lane < row_sub, jnp.broadcast_to(opens, square), 0), axis=1, keepdims=True)
    mine = row_sub[:, 0:1]
    place = jnp.where(mine < local_rows, base * GROUP + prior_sub, -1)
    wide = (slots, width)
    spot = lax.broadcasted_iota(jnp.int32, wide, 1)
    hit = jnp.broadcast_to(place, wide) == spot
    slot = lax.broadcasted_iota(jnp.int32, wide, 0)

    def total(value):
        return jnp.sum(jnp.where(hit, value, 0), axis=0, keepdims=True)

    plan_vector[0:1, :] = total(slot)
    plan_vector[1:2, :] = zero_block + total(jnp.broadcast_to(col_sub - zero_block, wide))
    plan_vector[2:3, :] = 1 - total(jnp.broadcast_to(jnp.where(prior_sub == 0, 1, 0), wide))
    here = jnp.broadcast_to(mine, wide) == spot
    unit = jnp.broadcast_to(lax.shift_right_arithmetic(place, GROUP // 2), wide)
    last = jnp.max(jnp.where(here, unit, -1), axis=0, keepdims=True)
    plan_vector[3:4, :] = jnp.where(last < 0, units, last)


def kernel(n_row, n_col, n_x, units, rows_ref, cols_ref, demand, tile_hbm, out, tiles, panel_a, panel_b, products,
           packed, landed, first, plan_vector, plan, tile_sem, plan_sem, sx, rx, su, ru, sd, rd, sr, rr):
    n_z = n_col // n_x
    span, edge, columns = demand.shape
    zero_block = n_col * span
    depth = edge // CUTS
    pieces = span * CUTS
    row = lax.axis_index("row")
    col = lax.axis_index("col")
    z = col // n_x
    x = col % n_x
    peer = z * n_x + (n_x - 1 - x)
    up_ok = z < n_z - 1
    down_ok = z > 0

    tile_copy = pltpu.make_async_copy(tile_hbm.at[0, 0], tiles, tile_sem)
    tile_copy.start()

    barrier = pltpu.get_barrier_semaphore()

    def greet(r, c):
        pl.semaphore_signal(barrier, inc=1, device_id=(r, c), device_id_type=MESH)

    for step in range(1, n_row):
        greet((row + step) % n_row, col)
    if n_x > 1:
        greet(row, peer)
    pl.when(up_ok)(lambda: greet(row, col + n_x))
    pl.when(down_ok)(lambda: greet(row, col - n_x))

    for panel in (panel_a, panel_b):
        panel[zero_block] = jnp.zeros((edge, columns), panel.dtype)
    products[units] = jnp.zeros((edge, columns), jnp.float32)
    panel_a[pl.ds(col * span, span)] = demand[...]
    greeted = n_row - 1 + (1 if n_x > 1 else 0) + up_ok.astype(jnp.int32) + down_ok.astype(jnp.int32)
    pl.semaphore_wait(barrier, greeted)

    def remote(src, dst, send, recv, target):
        return pltpu.make_async_remote_copy(
            src_ref=src, dst_ref=dst, send_sem=send, recv_sem=recv, device_id=(row, target), device_id_type=MESH
        )

    def gather(turn, own, panel, ready):
        def piece(ref, tile, p):
            return ref.at[tile + p // CUTS, pl.ds((p % CUTS) * depth, depth)]

        def cross(c, offset, p, src=None):
            at = (turn, offset + n_z - 1, p)
            there = piece(panel, c * span, p)
            return remote(there if src is None else piece(src, 0, p), there, sx.at[at], rx.at[at], peer)

        def upward(c, away, p, src=None):
            there = piece(panel, c * span, p)
            here = there if src is None else piece(src, 0, p)
            return remote(here, there, su.at[turn, away, p], ru.at[turn, away + 1, p], col + n_x)

        def downward(c, away, p, src=None):
            there = piece(panel, c * span, p)
            here = there if src is None else piece(src, 0, p)
            return remote(here, there, sd.at[turn, away, p], rd.at[turn, away + 1, p], col - n_x)

        def arrived(c, sem, away, p):
            there = piece(panel, c * span, p)
            remote(there, there, sem.at[turn, away, p], sem.at[turn, away, p], peer).wait_recv()

        for p in range(pieces):
            if p % CUTS == 0:
                ready(p // CUTS)
            pl.when(up_ok)(lambda: upward(col, 0, p, own).start())
            pl.when(down_ok)(lambda: downward(col, 0, p, own).start())
            if n_x > 1:
                cross(col, 0, p, own).start()
        ready(span)
        for away in range(1, n_z):
            for p in range(pieces):

                @pl.when(z >= away)
                def _():
                    c = col - away * n_x
                    arrived(c, ru, away, p)
                    if away + 1 < n_z:
                        pl.when(up_ok)(lambda: upward(c, away, p).start())
                    if n_x > 1:
                        cross(c, -away, p).start()

                @pl.when(z + away < n_z)
                def _():
                    c = col + away * n_x
                    arrived(c, rd, away, p)
                    if away + 1 < n_z:
                        pl.when(down_ok)(lambda: downward(c, away, p).start())
                    if n_x > 1:
                        cross(c, away, p).start()

        if n_x > 1:
            for p in range(pieces):
                cross(peer, 0, p).wait_recv()
                for away in range(1, n_z):
                    pl.when(z >= away)(lambda: cross(peer - away * n_x, -away, p).wait_recv())
                    pl.when(z + away < n_z)(lambda: cross(peer + away * n_x, away, p).wait_recv())

        def drain():
            for p in range(pieces):
                pl.when(up_ok)(lambda: upward(col, 0, p, own).wait_send())
                pl.when(down_ok)(lambda: downward(col, 0, p, own).wait_send())
                if n_x > 1:
                    cross(col, 0, p, own).wait_send()
                for away in range(1, n_z):

                    @pl.when(z >= away)
                    def _():
                        c = col - away * n_x
                        if n_x > 1:
                            cross(c, -away, p).wait_send()
                        if away + 1 < n_z:
                            pl.when(up_ok)(lambda: upward(c, away, p).wait_send())

                    @pl.when(z + away < n_z)
                    def _():
                        c = col + away * n_x
                        if n_x > 1:
                            cross(c, away, p).wait_send()
                        if away + 1 < n_z:
                            pl.when(down_ok)(lambda: downward(c, away, p).wait_send())

        return drain

    def compute(panel):
        def body(step, total):
            for part in range(UNROLL):
                unit = step * UNROLL + part
                left = [tiles[plan[0, unit * GROUP + k]] for k in range(GROUP)]
                right = [panel[plan[1, unit * GROUP + k]] for k in range(GROUP)]
                keep = plan[2, unit * GROUP].astype(jnp.float32)
                total = total * keep + jnp.dot(
                    jnp.concatenate(left, axis=1), jnp.concatenate(right, axis=0), preferred_element_type=jnp.float32
                )
                products[unit] = total
            return total

        lax.fori_loop(0, units // UNROLL, body, jnp.zeros((edge, columns), jnp.float32))

    def send(turn, step, k):
        r = (row + step) % n_row
        return pltpu.make_async_remote_copy(
            src_ref=packed.at[turn, r * span + k],
            dst_ref=landed.at[turn, step - 1, k],
            send_sem=sr.at[turn, step - 1, k],
            recv_sem=rr.at[turn, step - 1, k],
            device_id=(r, col),
            device_id_type=MESH,
        )

    def scatter(turn):
        steps = sorted(range(1, n_row), key=lambda step: abs(step - n_row // 2))
        for k in range(span):
            for step in steps:
                r = (row + step) % n_row
                packed[turn, r * span + k] = products[plan[3, r * span + k]].astype(packed.dtype)
                send(turn, step, k).start()

        def drain():
            for k in range(span):
                for step in steps:
                    send(turn, step, k).wait_send()

        return drain

    def collect(turn, k):
        value = products[plan[3, row * span + k]]
        for step in range(1, n_row):
            send(turn, step, k).wait_recv()
            value = value + landed[turn, step - 1, k].astype(jnp.float32)
        return value.astype(first.dtype)

    def ready_a(k):
        if k == span:
            schedule(rows_ref, cols_ref, plan_vector, n_row * span, zero_block, units)
            plan_copy = pltpu.make_async_copy(plan_vector, plan, plan_sem)
            plan_copy.start()
            plan_copy.wait()

    def ready_b(k):
        if k < span:
            value = collect(0, k)
            first[k] = value
            panel_b[col * span + k] = value

    drains = [gather(0, demand, panel_a, ready_a)]
    tile_copy.wait()
    compute(panel_a)
    drains.append(scatter(0))
    drains.append(gather(1, first, panel_b, ready_b))
    compute(panel_b)
    drains.append(scatter(1))
    for k in range(span):
        value = collect(1, k)
        out[k] = (
            demand[k].astype(jnp.float32) + first[k].astype(jnp.float32) + value.astype(jnp.float32)
        ).astype(out.dtype)
    for drain in drains:
        drain()


def body(n_row, n_col, demand, tile_data, tile_row, tile_col):
    slots, edge = tile_data.shape[2], tile_data.shape[-1]
    columns = demand.shape[1]
    span = demand.shape[0] // edge
    local_rows = n_row * span
    n_x = 2 if n_col % 2 == 0 else 1
    n_z = n_col // n_x
    units = (slots + local_rows * (GROUP - 1)) // GROUP
    units = -(-units // UNROLL) * UNROLL
    width = -(-max(units * GROUP, local_rows) // 128) * 128
    pieces = span * CUTS
    dma = pltpu.SemaphoreType.DMA
    vmem = pl.BlockSpec(memory_space=pltpu.VMEM)
    result = pl.pallas_call(
        functools.partial(kernel, n_row, n_col, n_x, units),
        out_shape=jax.ShapeDtypeStruct((span, edge, columns), demand.dtype),
        in_specs=[vmem, vmem, vmem, pl.BlockSpec(memory_space=pl.ANY)],
        out_specs=vmem,
        scratch_shapes=[
            pltpu.VMEM((slots, edge, edge), tile_data.dtype),
            pltpu.VMEM((n_col * span + 1, edge, columns), demand.dtype),
            pltpu.VMEM((n_col * span + 1, edge, columns), demand.dtype),
            pltpu.VMEM((units + 1, edge, columns), jnp.float32),
            pltpu.VMEM((2, local_rows, edge, columns), demand.dtype),
            pltpu.VMEM((2, n_row - 1, span, edge, columns), demand.dtype),
            pltpu.VMEM((span, edge, columns), demand.dtype),
            pltpu.VMEM((8, width), jnp.int32),
            pltpu.SMEM((8, width), jnp.int32),
            dma,
            dma,
            dma((2, 2 * n_z - 1, pieces)),
            dma((2, 2 * n_z - 1, pieces)),
            dma((2, n_z + 1, pieces)),
            dma((2, n_z + 1, pieces)),
            dma((2, n_z + 1, pieces)),
            dma((2, n_z + 1, pieces)),
            dma((2, n_row - 1, span)),
            dma((2, n_row - 1, span)),
        ],
        compiler_params=pltpu.CompilerParams(
            collective_id=0, has_side_effects=True, vmem_limit_bytes=56 * 1024 * 1024
        ),
    )(tile_row[0], tile_col[0], demand.reshape(span, edge, columns), tile_data)
    return result.reshape(demand.shape)


def solution(mesh):
    placed = (
        P(("row", "col"), None),
        P("row", "col", None, None, None),
        P("row", "col", None),
        P("row", "col", None),
    )
    return jax.shard_map(
        functools.partial(body, mesh.shape["row"], mesh.shape["col"]),
        mesh=mesh, in_specs=placed, out_specs=P(("row", "col"), None), check_vma=False,
    )
```

time: 186 us -> 47.6 us (0.26)
  blocking collectives: 66.5 us -> 0 us
  Pallas kernels: 0 us -> 45.9 us
  waiting for transfers between devices: 42.9 us -> 0 us
  local copies, waits for them, and re-layouts: 27.1 us -> 1.54 us
  matrix products: 24.6 us -> 0 us
  between operations: 13.4 us -> 0.01 us
  other arithmetic: 11 us -> 0 us
    all_gather x2 -> x0, blocking collectives: 66.5 us -> none  [multiply(): gathered = lax.all_gather(panel_piece, 'col', axis=0, tiled=True)]
    pallas_call x0 -> x1, Pallas kernels: none -> 45.9 us  [body(): pl.pallas_call(functools.partial(kernel, n_row, n_col, n_x, units), out_s...]
    reduce_scatter x2 -> x0, waiting for transfers between devices: 42.9 us -> none  [multiply(): lax.psum_scatter(partial_value.astype(jnp.bfloat16), 'row', scatter_dimen...]
    dot_general x6 -> x0, matrix products: 24.6 us -> none  [the longest x2 19.8 us: multiply(): jnp.einsum('stk,skc->stc', tile_block, picked, preferred_element_type=jnp...]
    dot_general x2 -> x0, local copies, waits for them, and re-layouts: 18.8 us -> none  [multiply(): jnp.einsum('stk,skc->stc', tile_block, picked, preferred_element_type=jnp...]
    convert_element_type x3 -> x0, other arithmetic: 9.63 us -> none  [the longest x2 8.06 us: multiply(): lower = (products - upper.astype(jnp.float32)).astype(jnp.bfloat16)]
    gather x2 -> x0, local copies, waits for them, and re-layouts: 6.08 us -> none  [multiply(): picked = jnp.take(blocks, slot_cols, axis=0)]
    convert_element_type x2 -> x0, local copies, waits for them, and re-layouts: 2.16 us -> none  [multiply(): partial_value.astype(jnp.bfloat16)]
  transfers between devices with their start and end apart: 2 -> 0, of which waited for: 2 -> 0; matrix products, arithmetic and copies ran while one was open for 0% -> 0% of each run, Pallas kernels for 0% -> 0%
where the time goes in v2:
time: 47.6 us; the launch traced here: 47.4 us
  Pallas kernels  45.9 us (96%)
  local copies, waits for them, and re-layouts  1.54 us (3%)
    pallas_call x1, Pallas kernels, body(): pl.pallas_call(functools.partial(kernel, n_row, n_col, n_x, units), out_s...  45.9 us
    unnamed x1, local copies, waits for them, and re-layouts  1.54 us

profile of v2, /device:TPU:0, one launch (start us, length us, event | category | flops | bytes accessed | tf_op | source)
XLA Modules:
  0.0 47.4 jit_solution(6259182087056835452)
XLA Ops:
  0.0 45.9 %shard_map.46 = bf16[3,128,128]{2,1,0:T(8,128)(2,1)} custom-call(s32[1,128]{1,0:T(1,128)} %bitcast.6, s32[1,128]{1,0:T(1,128)} %bitcast.7, bf16[3,128,128]{2,1,0:T(8,128)(2,1)} %bitcast.5, bf16[1,1,128,128,128]{4,3,2,1,0:T(8,128)(2,1)} %tile_hbm.1), custom_call_target="tpu_custom_call" | custom-call | tf_op jit(solution)/shard_map/pallas_call | solution.py:266
  45.9 1.5 %copy.6 = bf16[384,128]{1,0:T(8,128)(2,1)} copy(bf16[384,128]{1,0:T(8,128)(2,1)} %bitcast.4) | data formatting | bytes 196608
